TPU v7x, 16 devices: a 4x2x1 block of a 4x4x8 slice. The times are simulated.
16 devices in a mesh: dp: 2 (over y, z), tp: 8 (over x, core).
Axes of the slice: x: 4, y: 2, z: 1, core: 2. Of those that a mesh axis runs over, the one named last changes fastest.
The devices are a block of a 4x4x8 slice.
Arguments:
- x: bfloat16 [512, 3072], P(('dp', 'tp')), parts along dimension 0
- grad_y: bfloat16 [512, 3072], P(('dp', 'tp')), parts along dimension 0
- gain_attn: float32 [2, 3072], replicated
- gain_mlp: float32 [2, 3072], replicated
- w_qkv: bfloat16 [2, 3072, 5120], P(None, None, 'tp')
- w_out: bfloat16 [2, 3072, 3072], P(None, 'tp')
- w_gate: bfloat16 [2, 3072, 8192], P(None, None, 'tp')
- w_up: bfloat16 [2, 3072, 8192], P(None, None, 'tp')
- w_down: bfloat16 [2, 8192, 3072], P(None, 'tp')
Outputs:
- output 1: bfloat16 [512, 3072], P(('dp', 'tp')), parts along dimension 0
- output 2: bfloat16 [512, 3072], P(('dp', 'tp')), parts along dimension 0
- output 3: bfloat16 [4, 3072, 5120], P('dp', None, 'tp'), parts along dimension 0
- output 4: bfloat16 [4, 3072, 3072], P('dp', 'tp'), parts along dimension 0
- output 5: bfloat16 [4, 3072, 8192], P('dp', None, 'tp'), parts along dimension 0
- output 6: bfloat16 [4, 3072, 8192], P('dp', None, 'tp'), parts along dimension 0
- output 7: bfloat16 [4, 8192, 3072], P('dp', 'tp'), parts along dimension 0
- output 8: float32 [4, 3072], P('dp'), parts along dimension 0
- output 9: float32 [4, 3072], P('dp'), parts along dimension 0
There are 2 independent parts. A program takes and returns all parts, laid end to end along the dimension named above; an argument that names none is the same for every part.
All inputs are finite; a program needn't handle non-finite values.
Results may differ from a plain program's by a relative error of at most 0.017233.
Values are sent between devices in bfloat16 or wider.
A program may use at most 768 MiB of HBM per device.

v0:
```python
import jax
import jax.numpy as jnp
from jax import lax
from jax.sharding import PartitionSpec as P

HEAD_DIM = 128
NORM_EPS = 1e-5


def rms_norm(hidden_in, gain_vec):
    hidden_f = hidden_in.astype(jnp.float32)
    inv_rms = lax.rsqrt(jnp.mean(hidden_f * hidden_f, axis=-1, keepdims=True) + NORM_EPS)
    return (hidden_f * inv_rms * gain_vec).astype(jnp.bfloat16)


def swiglu(gate_act, up_act):
    return (jax.nn.silu(gate_act.astype(jnp.float32)) * up_act.astype(jnp.float32)).astype(jnp.bfloat16)


def contract(left_op, right_op, eq_form):
    return jnp.einsum(eq_form, left_op, right_op, preferred_element_type=jnp.float32)


def gather_rows(row_shard):
    return lax.all_gather(row_shard, 'tp', axis=0, tiled=True)


def scatter_rows(part_sum):
    return lax.psum_scatter(part_sum, 'tp', scatter_dimension=0, tiled=True).astype(jnp.bfloat16)


def attention_core(full_in, w_qkv, kv_local, group_size):
    seq_len = full_in.shape[0]
    qkv_out = jnp.dot(full_in, w_qkv, preferred_element_type=jnp.float32).astype(jnp.bfloat16)
    blocks = qkv_out.reshape(seq_len, kv_local, group_size + 2, HEAD_DIM)
    queries = blocks[:, :, :group_size]
    key_rows = blocks[:, :, group_size]
    value_rows = blocks[:, :, group_size + 1]
    scores = contract(queries, key_rows, 'ikqh,jkh->kqij') * HEAD_DIM ** -0.5
    positions = jnp.arange(seq_len)
    causal = positions[:, None] >= positions[None, :]
    prob_f32 = jax.nn.softmax(jnp.where(causal, scores, -1e30), axis=-1)
    prob_low = prob_f32.astype(jnp.bfloat16)
    heads_out = contract(prob_low, value_rows, 'kqij,jkh->ikqh').astype(jnp.bfloat16)
    heads_out = heads_out.reshape(seq_len, kv_local * group_size * HEAD_DIM)
    return queries, key_rows, value_rows, prob_f32, prob_low, heads_out


def mlp_core(full_mid, w_gate, w_up):
    gate_act = jnp.dot(full_mid, w_gate, preferred_element_type=jnp.float32).astype(jnp.bfloat16)
    up_act = jnp.dot(full_mid, w_up, preferred_element_type=jnp.float32).astype(jnp.bfloat16)
    return gate_act, up_act, swiglu(gate_act, up_act)


def layer_forward(hidden_in, weights, kv_local, group_size):
    gain_attn, gain_mlp, w_qkv, w_out, w_gate, w_up, w_down = weights
    full_in = gather_rows(rms_norm(hidden_in, gain_attn))
    attn_parts = attention_core(full_in, w_qkv, kv_local, group_size)
    hidden_mid = hidden_in + scatter_rows(jnp.dot(attn_parts[5], w_out, preferred_element_type=jnp.float32))
    full_mid = gather_rows(rms_norm(hidden_mid, gain_mlp))
    mlp_parts = mlp_core(full_mid, w_gate, w_up)
    layer_out = hidden_mid + scatter_rows(jnp.dot(mlp_parts[2], w_down, preferred_element_type=jnp.float32))
    return layer_out, (full_in, attn_parts, hidden_mid, full_mid, mlp_parts)


def layer_backward(hidden_in, saved_acts, d_out, weights):
    gain_attn, gain_mlp, w_qkv, w_out, w_gate, w_up, w_down = weights
    full_in, attn_parts, hidden_mid, full_mid, mlp_parts = saved_acts
    queries, key_rows, value_rows, prob_f32, prob_low, heads_out = attn_parts
    gate_act, up_act, gated_act = mlp_parts
    seq_len, kv_local, group_size = queries.shape[0], queries.shape[1], queries.shape[2]
    d_down_full = gather_rows(d_out)
    grad_down = contract(gated_act, d_down_full, 'sf,sd->fd').astype(jnp.bfloat16)
    d_gated = contract(d_down_full, w_down, 'sd,fd->sf').astype(jnp.bfloat16)
    _, swiglu_pull = jax.vjp(swiglu, gate_act, up_act)
    d_gate, d_up = swiglu_pull(d_gated)
    grad_gate = contract(full_mid, d_gate, 'sd,sf->df').astype(jnp.bfloat16)
    grad_up = contract(full_mid, d_up, 'sd,sf->df').astype(jnp.bfloat16)
    d_mid = scatter_rows(contract(d_gate, w_gate, 'sf,df->sd') + contract(d_up, w_up, 'sf,df->sd'))
    _, norm_mid_pull = jax.vjp(rms_norm, hidden_mid, gain_mlp)
    d_norm_mid, grad_gain_mlp = norm_mid_pull(d_mid)
    d_hidden_mid = d_out + d_norm_mid
    d_attn_full = gather_rows(d_hidden_mid)
    grad_out = contract(heads_out, d_attn_full, 'sr,sd->rd').astype(jnp.bfloat16)
    d_heads = contract(d_attn_full, w_out, 'sd,rd->sr').astype(jnp.bfloat16).reshape(seq_len, kv_local, group_size, HEAD_DIM)
    d_prob = contract(d_heads, value_rows, 'ikqh,jkh->kqij')
    d_values = contract(prob_low, d_heads, 'kqij,ikqh->jkh').astype(jnp.bfloat16)
    d_scores = (prob_f32 * (d_prob - jnp.sum(d_prob * prob_f32, axis=-1, keepdims=True)) * HEAD_DIM ** -0.5).astype(jnp.bfloat16)
    d_queries = contract(d_scores, key_rows, 'kqij,jkh->ikqh').astype(jnp.bfloat16)
    d_keys = contract(d_scores, queries, 'kqij,ikqh->jkh').astype(jnp.bfloat16)
    d_qkv = jnp.concatenate([d_queries, d_keys[:, :, None], d_values[:, :, None]], axis=2).reshape(seq_len, -1)
    grad_qkv = contract(full_in, d_qkv, 'sd,sc->dc').astype(jnp.bfloat16)
    d_in = scatter_rows(contract(d_qkv, w_qkv, 'sc,dc->sd'))
    _, norm_in_pull = jax.vjp(rms_norm, hidden_in, gain_attn)
    d_norm_in, grad_gain_attn = norm_in_pull(d_in)
    return d_hidden_mid + d_norm_in, (grad_gain_attn, grad_gain_mlp, grad_qkv, grad_out, grad_gate, grad_up, grad_down)


def solution(mesh):
    row_spec = P(('dp', 'tp'), None)
    col_spec = P(None, None, 'tp')
    mid_spec = P(None, 'tp', None)
    in_specs = (row_spec, row_spec, P(None, None), P(None, None), col_spec, mid_spec, col_spec, col_spec, mid_spec)
    out_specs = (row_spec, row_spec, P('dp', None, 'tp'), P('dp', 'tp', None), P('dp', None, 'tp'), P('dp', None, 'tp'), P('dp', 'tp', None), P('dp', None), P('dp', None))

    def device_step(x, grad_y, gain_attn, gain_mlp, w_qkv, w_out, w_gate, w_up, w_down):
        all_weights = (gain_attn, gain_mlp, w_qkv, w_out, w_gate, w_up, w_down)
        num_layers = w_qkv.shape[0]
        rows_local = w_out.shape[1]
        kv_local = (w_qkv.shape[2] - rows_local) // (2 * HEAD_DIM)
        group_size = rows_local // (kv_local * HEAD_DIM)
        layer_inputs = [x]
        for layer_idx in range(num_layers):
            weights = tuple(weight[layer_idx] for weight in all_weights)
            layer_out, _ = layer_forward(layer_inputs[-1], weights, kv_local, group_size)
            layer_inputs.append(layer_out)
        d_hidden = grad_y
        layer_grads = [None] * num_layers
        for layer_idx in reversed(range(num_layers)):
            weights = tuple(weight[layer_idx] for weight in all_weights)
            kept_in, d_hidden = lax.optimization_barrier((layer_inputs[layer_idx], d_hidden))
            _, saved_acts = layer_forward(kept_in, weights, kv_local, group_size)
            d_hidden, layer_grads[layer_idx] = layer_backward(kept_in, saved_acts, d_hidden, weights)
        stacked = [jnp.stack([grads[kind_idx] for grads in layer_grads]) for kind_idx in range(7)]
        gain_grads = lax.psum(jnp.stack([stacked[0], stacked[1]]), 'tp')
        return (layer_inputs[-1], d_hidden, stacked[2], stacked[3], stacked[4], stacked[5], stacked[6], gain_grads[0], gain_grads[1])

    return jax.shard_map(device_step, mesh=mesh, in_specs=in_specs, out_specs=out_specs, check_vma=False)
```

profile of v0, /device:TPU:112, one launch (start us, length us, event | category | flops | bytes accessed | tf_op | source)
XLA Modules:
  0.0 712.7 jit_solution(7998521330339477433)
XLA Ops:
  11.1 23.1 %all-gather.13.cloned.1.call-done = bf16[256,3072]{1,0:T(8,128)(2,1)} async-done(((bf16[32,3072]{1,0:T(8,128)(2,1)}), bf16[256,3072]{1,0:T(8,128)(2,1)}) %all-gather.13.cloned.1.call-update) | async-done | bytes 1572880 | tf_op jit(solution)/shard_map/all_gather | solution.py:25
  43.7 32.0 %reduce-scatter.11.cloned.1.call-done = f32[32,3072]{1,0:T(8,128)} async-done(((f32[256,3072]{1,0:T(8,128)}), f32[32,3072]{1,0:T(8,128)}) %reduce-scatter.11.cloned.1.call-update) | async-done | bytes 393232 | tf_op jit(solution)/shard_map/reduce_scatter | solution.py:29
  77.9 19.1 %all-gather.15.cloned.1.call-done = bf16[256,3072]{1,0:T(8,128)(2,1)} async-done(((bf16[32,3072]{1,0:T(8,128)(2,1)}), bf16[256,3072]{1,0:T(8,128)(2,1)}) %all-gather.15.cloned.1.call-update) | async-done | bytes 1572880 | tf_op jit(solution)/shard_map/all_gather | solution.py:25
  102.1 9.8 %fusion.18 = f32[256,3072]{1,0:T(8,128)} fusion(bf16[2,1024,3072]{2,1,0:T(8,128)(2,1)} %param.17, bf16[256,3072]{1,0:T(8,128)(2,1)S(1)} %copy-done.26, bf16[2,3072,1024]{2,1,0:T(8,128)(2,1)} %param.16, bf16[256,1024]{1,0:T(8,128)(2,1)S(1)} %fusion.94), kind=kOutput, calls=%fused_computation.22 | convolution fusion | flops 3223584768 | bytes 17825792 | tf_op jit(solution)/shard_map/dot_general | solution.py:62
  112.1 32.1 %reduce-scatter.13.cloned.1.call-done = f32[32,3072]{1,0:T(8,128)} async-done(((f32[256,3072]{1,0:T(8,128)}), f32[32,3072]{1,0:T(8,128)}) %reduce-scatter.13.cloned.1.call-update) | async-done | bytes 393232 | tf_op jit(solution)/shard_map/reduce_scatter | solution.py:29
  146.5 19.1 %all-gather.23.cloned.1.call-done = bf16[256,3072]{1,0:T(8,128)(2,1)} async-done(((bf16[32,3072]{1,0:T(8,128)(2,1)}), bf16[256,3072]{1,0:T(8,128)(2,1)}) %all-gather.23.cloned.1.call-update) | async-done | bytes 1572880 | tf_op jit(solution)/shard_map/all_gather | solution.py:25
  175.7 31.3 %reduce-scatter.19.cloned.1.call-done = f32[32,3072]{1,0:T(8,128)} async-done(((f32[256,3072]{1,0:T(8,128)}), f32[32,3072]{1,0:T(8,128)}) %reduce-scatter.19.cloned.1.call-update) | async-done | bytes 393232 | tf_op jit(solution)/shard_map/reduce_scatter | solution.py:29
  209.4 18.3 %all-gather.21.cloned.1.call-done = bf16[256,3072]{1,0:T(8,128)(2,1)} async-done(((bf16[32,3072]{1,0:T(8,128)(2,1)}), bf16[256,3072]{1,0:T(8,128)(2,1)}) %all-gather.21.cloned.1.call-update) | async-done | bytes 1572880 | tf_op jit(solution)/shard_map/all_gather | solution.py:25
  233.6 16.7 %all-gather.25.cloned.1.call-done = bf16[256,3072]{1,0:T(8,128)(2,1)} async-done(((bf16[32,3072]{1,0:T(8,128)(2,1)}), bf16[256,3072]{1,0:T(8,128)(2,1)}) %all-gather.25.cloned.1.call-update) | async-done | bytes 1572880 | tf_op jit(solution)/shard_map/all_gather | solution.py:25
  270.0 32.2 %reduce-scatter.21.cloned.1.call-done = f32[32,3072]{1,0:T(8,128)} async-done(((f32[256,3072]{1,0:T(8,128)}), f32[32,3072]{1,0:T(8,128)}) %reduce-scatter.21.cloned.1.call-update) | async-done | bytes 393232 | tf_op jit(solution)/shard_map/reduce_scatter | solution.py:29
  306.4 18.6 %all-gather.27.cloned.1.call-done = bf16[256,3072]{1,0:T(8,128)(2,1)} async-done(((bf16[32,3072]{1,0:T(8,128)(2,1)}), bf16[256,3072]{1,0:T(8,128)(2,1)}) %all-gather.27.cloned.1.call-update) | async-done | bytes 1572880 | tf_op jit(solution)/shard_map/all_gather | solution.py:25
  335.1 32.1 %reduce-scatter.23.cloned.1.call-done = f32[32,3072]{1,0:T(8,128)} async-done(((f32[256,3072]{1,0:T(8,128)}), f32[32,3072]{1,0:T(8,128)}) %reduce-scatter.23.cloned.1.call-update) | async-done | bytes 393232 | tf_op jit(solution)/shard_map/reduce_scatter | solution.py:29
  372.6 19.1 %all-gather.31.cloned.1.call-done = bf16[256,3072]{1,0:T(8,128)(2,1)} async-done(((bf16[32,3072]{1,0:T(8,128)(2,1)}), bf16[256,3072]{1,0:T(8,128)(2,1)}) %all-gather.31.cloned.1.call-update) | async-done | bytes 1572880 | tf_op jit(solution)/shard_map/all_gather | solution.py:25
  402.4 30.9 %reduce-scatter.25.cloned.1.call-done = f32[32,3072]{1,0:T(8,128)} async-done(((f32[256,3072]{1,0:T(8,128)}), f32[32,3072]{1,0:T(8,128)}) %reduce-scatter.25.cloned.1.call-update) | async-done | bytes 393232 | tf_op jit(solution)/shard_map/reduce_scatter | solution.py:29
  435.4 18.9 %all-gather.17.cloned.1.call-done = bf16[256,3072]{1,0:T(8,128)(2,1)} async-done(((bf16[32,3072]{1,0:T(8,128)(2,1)}), bf16[256,3072]{1,0:T(8,128)(2,1)}) %all-gather.17.cloned.1.call-update) | async-done | bytes 1572880 | tf_op jit(solution)/shard_map/all_gather | solution.py:25
  463.8 12.3 %all-gather.29.cloned.1.call-done = bf16[256,3072]{1,0:T(8,128)(2,1)} async-done(((bf16[32,3072]{1,0:T(8,128)(2,1)}), bf16[256,3072]{1,0:T(8,128)(2,1)}) %all-gather.29.cloned.1.call-update) | async-done | bytes 1572880 | tf_op jit(solution)/shard_map/all_gather | solution.py:25
  482.0 16.5 %all-gather.33.cloned.1.call-done = bf16[256,3072]{1,0:T(8,128)(2,1)} async-done(((bf16[32,3072]{1,0:T(8,128)(2,1)}), bf16[256,3072]{1,0:T(8,128)(2,1)}) %all-gather.33.cloned.1.call-update) | async-done | bytes 1572880 | tf_op jit(solution)/shard_map/all_gather | solution.py:25
  517.6 15.7 %reduce-scatter.15.cloned.1.call-done = f32[32,3072]{1,0:T(8,128)} async-done(((f32[256,3072]{1,0:T(8,128)}), f32[32,3072]{1,0:T(8,128)}) %reduce-scatter.15.cloned.1.call-update) | async-done | bytes 393232 | tf_op jit(solution)/shard_map/reduce_scatter | solution.py:29
  535.4 31.3 %reduce-scatter.27.cloned.1.call-done = f32[32,3072]{1,0:T(8,128)} async-done(((f32[256,3072]{1,0:T(8,128)}), f32[32,3072]{1,0:T(8,128)}) %reduce-scatter.27.cloned.1.call-update) | async-done | bytes 393232 | tf_op jit(solution)/shard_map/reduce_scatter | solution.py:29
  570.0 17.9 %all-gather.19.cloned.1.call-done = bf16[256,3072]{1,0:T(8,128)(2,1)} async-done(((bf16[32,3072]{1,0:T(8,128)(2,1)}), bf16[256,3072]{1,0:T(8,128)(2,1)}) %all-gather.19.cloned.1.call-update) | async-done | bytes 1572880 | tf_op jit(solution)/shard_map/all_gather | solution.py:25
  593.8 10.4 %fusion.2 = f32[256,3072]{1,0:T(8,128)} fusion(bf16[2,1024,3072]{2,1,0:T(8,128)(2,1)} %param.17, bf16[256,3072]{1,0:T(8,128)(2,1)} %all-gather.19.cloned.1.call-done, bf16[2,3072,1024]{2,1,0:T(8,128)(2,1)} %param.16, bf16[256,1024]{1,0:T(8,128)(2,1)} %fusion.115), kind=kOutput, calls=%fused_computation.6 | convolution fusion | flops 3223584768 | bytes 17825792 | tf_op jit(solution)/shard_map/dot_general | solution.py:62
  641.3 9.3 %pad_maximum_fusion.2 = bf16[2,1024,3072]{2,1,0:T(8,128)(2,1)} fusion(bf16[1,1024,3072]{2,1,0:T(8,128)(2,1)S(1)} %convert_bitcast_fusion, bf16[1,1024,3072]{2,1,0:T(8,128)(2,1)} %convert_bitcast_fusion.1), kind=kLoop, calls=%fused_computation.2 | loop fusion | flops 6291456 | bytes 25165824 | tf_op jit(solution)/shard_map/stack | solution.py:124
  650.6 8.8 %pad_maximum_fusion = (bf16[2,3072,1024]{2,1,0:T(8,128)(2,1)}, bf16[2,3072,1024]{2,1,0:T(8,128)(2,1)}) fusion(bf16[1,3072,1024]{2,1,0:T(8,128)(2,1)S(1)} %convert_bitcast_fusion.4, bf16[1,3072,1024]{2,1,0:T(8,128)(2,1)S(1)} %convert_bitcast_fusion.5, bf16[1,3072,1024]{2,1,0:T(8,128)(2,1)S(1)} %bitcast.429, bf16[1,3072,1024]{2,1,0:T(8,128)(2,1)S(1)} %convert_bitcast_fusion.3), kind=kLoop, calls=%fused_computation | loop fusion | flops 12582912 | bytes 50331648 | tf_op jit(solution)/shard_map/stack | solution.py:124
  679.2 24.0 %psum.7 = f32[2,2,3072]{2,1,0:T(2,128)S(1)} all-reduce(f32[2,2,3072]{2,1,0:T(2,128)S(1)} %pad_maximum_fusion.7), channel_id=1, replica_groups=mesh['dp'=2,'tp'=8] {'tp'}, use_global_device_ids=true, to_apply=%region_36.37 | all-reduce | flops 12288 | bytes 98304 | tf_op jit(solution)/shard_map/psum | solution.py:125
  (252 shorter events, 197.7 us)
Async XLA Ops:
  7.2 27.0 %all-gather.13.cloned.1.call-start = ((), (), s32[]{:S(2)}) async-start(), calls=%async_computation.10 | async-start | bytes 1769472 | tf_op jit(solution)/shard_map/all_gather | solution.py:25
  11.0 64.8 %reduce-scatter.11.cloned.1.call-start = ((), (), s32[]{:S(2)}) async-start(), calls=%async_computation.11 | async-start | bytes 3538944 | tf_op jit(solution)/shard_map/reduce_scatter | solution.py:29
  11.1 384.8 %copy-start.14 = (pred[256,256]{0,1:T(8,128)(4,1)}, pred[256,256]{0,1:T(8,128)(4,1)S(1)}, u32[]{:S(2)}) copy-start(pred[256,256]{0,1:T(8,128)(4,1)S(1)} %iota_compare_fusion) | copy-start | bytes 196612
  43.6 53.4 %all-gather.15.cloned.1.call-start = ((), (), s32[]{:S(2)}) async-start(), calls=%async_computation.12 | async-start | bytes 1769472 | tf_op jit(solution)/shard_map/all_gather | solution.py:25
  43.7 390.7 %copy-start.10 = (f32[1,3072]{1,0:T(1,128)}, f32[1,3072]{1,0:T(1,128)S(1)}, u32[]{:S(2)}) copy-start(f32[1,3072]{1,0:T(1,128)S(1)} %get-tuple-element.38) | copy-start | bytes 36868
  77.8 66.4 %reduce-scatter.13.cloned.1.call-start = ((), (), s32[]{:S(2)}) async-start(), calls=%async_computation.13 | async-start | bytes 3538944 | tf_op jit(solution)/shard_map/reduce_scatter | solution.py:29
  112.0 53.5 %all-gather.23.cloned.1.call-start = ((), (), s32[]{:S(2)}) async-start(), calls=%async_computation.19 | async-start | bytes 1769472 | tf_op jit(solution)/shard_map/all_gather | solution.py:25
  146.4 60.6 %reduce-scatter.19.cloned.1.call-start = ((), (), s32[]{:S(2)}) async-start(), calls=%async_computation.20 | async-start | bytes 3538944 | tf_op jit(solution)/shard_map/reduce_scatter | solution.py:29
  174.8 52.9 %all-gather.21.cloned.1.call-start = ((), (), s32[]{:S(2)}) async-start(), calls=%async_computation.18 | async-start | bytes 1769472 | tf_op jit(solution)/shard_map/all_gather | solution.py:25
  175.6 74.6 %all-gather.25.cloned.1.call-start = ((), (), s32[]{:S(2)}) async-start(), calls=%async_computation.21 | async-start | bytes 1769472 | tf_op jit(solution)/shard_map/all_gather | solution.py:25
  209.0 93.2 %reduce-scatter.21.cloned.1.call-start = ((), (), s32[]{:S(2)}) async-start(), calls=%async_computation.22 | async-start | bytes 3538944 | tf_op jit(solution)/shard_map/reduce_scatter | solution.py:29
  269.9 55.0 %all-gather.27.cloned.1.call-start = ((), (), s32[]{:S(2)}) async-start(), calls=%async_computation.23 | async-start | bytes 1769472 | tf_op jit(solution)/shard_map/all_gather | solution.py:25
  305.9 61.3 %reduce-scatter.23.cloned.1.call-start = ((), (), s32[]{:S(2)}) async-start(), calls=%async_computation.24 | async-start | bytes 3538944 | tf_op jit(solution)/shard_map/reduce_scatter | solution.py:29
  335.0 56.7 %all-gather.31.cloned.1.call-start = ((), (), s32[]{:S(2)}) async-start(), calls=%async_computation.26 | async-start | bytes 1769472 | tf_op jit(solution)/shard_map/all_gather | solution.py:25
  372.5 60.7 %reduce-scatter.25.cloned.1.call-start = ((), (), s32[]{:S(2)}) async-start(), calls=%async_computation.27 | async-start | bytes 3538944 | tf_op jit(solution)/shard_map/reduce_scatter | solution.py:29
  401.0 53.2 %all-gather.17.cloned.1.call-start = ((), (), s32[]{:S(2)}) async-start(), calls=%async_computation.14 | async-start | bytes 1769472 | tf_op jit(solution)/shard_map/all_gather | solution.py:25
  401.6 74.5 %all-gather.29.cloned.1.call-start = ((), (), s32[]{:S(2)}) async-start(), calls=%async_computation.25 | async-start | bytes 1769472 | tf_op jit(solution)/shard_map/all_gather | solution.py:25
  402.3 96.2 %all-gather.33.cloned.1.call-start = ((), (), s32[]{:S(2)}) async-start(), calls=%async_computation.28 | async-start | bytes 1769472 | tf_op jit(solution)/shard_map/all_gather | solution.py:25
  435.3 98.0 %reduce-scatter.15.cloned.1.call-start = ((), (), s32[]{:S(2)}) async-start(), calls=%async_computation.15 | async-start | bytes 3538944 | tf_op jit(solution)/shard_map/reduce_scatter | solution.py:29
  463.5 103.2 %reduce-scatter.27.cloned.1.call-start = ((), (), s32[]{:S(2)}) async-start(), calls=%async_computation.29 | async-start | bytes 3538944 | tf_op jit(solution)/shard_map/reduce_scatter | solution.py:29
  517.5 70.4 %all-gather.19.cloned.1.call-start = ((), (), s32[]{:S(2)}) async-start(), calls=%async_computation.16 | async-start | bytes 1769472 | tf_op jit(solution)/shard_map/all_gather | solution.py:25
  535.3 75.4 %all-gather.35.cloned.1.call-start = ((), (), s32[]{:S(2)}) async-start(), calls=%async_computation.30 | async-start | bytes 1769472 | tf_op jit(solution)/shard_map/all_gather | solution.py:25
  569.9 89.4 %reduce-scatter.17.cloned.1.call-start = ((), (), s32[]{:S(2)}) async-start(), calls=%async_computation.17 | async-start | bytes 3538944 | tf_op jit(solution)/shard_map/reduce_scatter | solution.py:29
  604.3 73.6 %reduce-scatter.29.cloned.1.call-start = ((), (), s32[]{:S(2)}) async-start(), calls=%async_computation.31 | async-start | bytes 3538944 | tf_op jit(solution)/shard_map/reduce_scatter | solution.py:29
  (45 other events, 789.6 us)
Sparse Core Ops, SparseCore 0:
  11.1 23.0 all-gather.12
  43.7 32.0 reduce-scatter.10
  77.9 19.0 all-gather.14
  112.1 32.0 reduce-scatter.12
  146.5 19.0 all-gather.22
  175.0 32.0 reduce-scatter.18
  208.6 19.0 all-gather.20
  229.8 20.3 all-gather.24
  270.1 32.0 reduce-scatter.20
  306.0 18.9 all-gather.26
  335.1 32.0 reduce-scatter.22
  372.6 19.0 all-gather.30
  401.1 32.0 reduce-scatter.24
  435.2 18.9 all-gather.16
  455.7 20.4 all-gather.28
  478.1 20.3 all-gather.32
  501.2 32.0 reduce-scatter.14
  536.0 30.6 reduce-scatter.26
  568.9 19.0 all-gather.18
  589.3 20.4 all-gather.34
  612.7 32.1 reduce-scatter.16
  647.2 30.6 reduce-scatter.28
where the time goes:
time: 722 us; the launch traced here: 713 us
  waiting for transfers between devices  445 us (62%)
  matrix products  165 us (23%)
  other arithmetic  55.7 us (8%)
  blocking collectives  24 us (3%)
  between operations  15.4 us (2%)
    reduce_scatter x10, waiting for transfers between devices, scatter_rows(): lax.psum_scatter(part_sum, 'tp', scatter_dimension=0, tiled=True)  243 us
    all_gather x12, waiting for transfers between devices, gather_rows(): return lax.all_gather(row_shard, 'tp', axis=0, tiled=True)  200 us
    dot_general x36, matrix products, contract(): jnp.einsum(eq_form, left_op, right_op, preferred_element_type=jnp.float32)  80.9 us
    another operation x4, other arithmetic, device_step(): jnp.stack([grads[kind_idx] for grads in layer_grads])  24.9 us
    psum x1, blocking collectives, device_step(): gain_grads = lax.psum(jnp.stack([stacked[0], stacked[1]]), 'tp')  24 us
    dot_general x4, matrix products, mlp_core(): jnp.dot(full_mid, w_gate, preferred_element_type=jnp.float32)  21.3 us
    dot_general x2, matrix products, layer_forward(): jnp.dot(mlp_parts[2], w_down, preferred_element_type=jnp.float32)  20.2 us
    dot_general x4, matrix products, layer_forward(): jnp.dot(attn_parts[5], w_out, preferred_element_type=jnp.float32)  17.4 us
  transfers between devices with their start and end apart: 22, of which 20 were waited for; matrix products, arithmetic and copies ran while one was open for 19% of the time, Pallas kernels for 0%

commit v1 on v0

v1 whole, which is shorter than its diff:
```python
import functools

import jax
import jax.numpy as jnp
from jax import lax
from jax.experimental import pallas as pl
from jax.experimental.pallas import tpu as pltpu
from jax.sharding import PartitionSpec as P

HEAD_DIM = 128
NORM_EPS = 1e-5
CORES = 2
MESH = pl.DeviceIdType.MESH
F32 = jnp.float32
BF16 = jnp.bfloat16
VMEM_LIMIT = 66_000_000
STEPS = 3
ANY = pl.BlockSpec(memory_space=pltpu.HBM)
VMEM_SPEC = pl.BlockSpec(memory_space=pltpu.VMEM)


def dot_nn(a, b):
    return lax.dot_general(a, b, (((1,), (0,)), ((), ())), preferred_element_type=F32)


def dot_nt(a, b):
    return lax.dot_general(a, b, (((1,), (1,)), ((), ())), preferred_element_type=F32)


def dot_tn(a, b):
    return lax.dot_general(a, b, (((0,), (0,)), ((), ())), preferred_element_type=F32)


class Links:
    def __init__(self, chips, send_sem, recv_sem):
        self.me = lax.axis_index('tp')
        self.chips = chips
        self.x = lax.div(self.me, CORES)
        self.c = lax.rem(self.me, CORES)
        self.xr = lax.rem(self.x + 1, chips)
        self.xl = lax.rem(self.x + chips - 1, chips)
        self.xo = lax.rem(self.x + 2, chips)
        self.right = self.xr * CORES + self.c
        self.left = self.xl * CORES + self.c
        self.sib = self.x * CORES + 1 - self.c
        self.send_sem, self.recv_sem, self.used, self.pending = send_sem, recv_sem, 0, []

    def enter(self, peers):
        barrier = pltpu.get_barrier_semaphore()
        for peer in peers:
            pl.semaphore_signal(barrier, inc=1, device_id={'tp': peer}, device_id_type=MESH)
        pl.semaphore_wait(barrier, len(peers))

    def others(self):
        size = self.chips * CORES
        return [lax.rem(self.me + step, size) for step in range(1, size)]

    def copy(self, src, dst, peer):
        copy = pltpu.make_async_remote_copy(
            src_ref=src, dst_ref=dst, send_sem=self.send_sem.at[self.used], recv_sem=self.recv_sem.at[self.used],
            device_id={'tp': peer}, device_id_type=MESH)
        self.used += 1
        copy.start()
        self.pending.append(copy)
        return copy

    def drain(self):
        for copy in self.pending:
            copy.wait_send()
        self.pending = []


class Gather:
    def __init__(self, links, full):
        self.links, self.full = links, full
        self.half = full.shape[3] // 2
        part_a, part_b = pl.ds(0, self.half), pl.ds(self.half, self.half)
        x, c = links.x, links.c
        self.a, self.b = part_a, part_b
        self.right_a = self.send(x, part_a, links.right)
        self.left_b = self.send(x, part_b, links.left)
        self.right_b = self.send(x, part_b, links.right)
        self.left_a = self.send(x, part_a, links.left)
        self.near = [links.copy(full.at[x, c], full.at[x, c], links.sib)]

    def send(self, chip, part, peer):
        ref = self.full.at[chip, self.links.c, :, part]
        return self.links.copy(ref, ref, peer)

    def relay(self):
        links = self.links
        self.right_a.wait_recv()
        relay_a = self.send(links.xl, self.a, links.right)
        self.near.append(self.send(links.xl, self.a, links.sib))
        self.left_b.wait_recv()
        relay_b = self.send(links.xr, self.b, links.left)
        self.near.append(self.send(links.xr, self.b, links.sib))
        self.right_b.wait_recv()
        self.near.append(self.send(links.xl, self.b, links.sib))
        self.left_a.wait_recv()
        self.near.append(self.send(links.xr, self.a, links.sib))
        self.far = (relay_a, relay_b)

    def finish(self):
        links = self.links
        self.far[0].wait_recv()
        self.near.append(self.send(links.xo, self.a, links.sib))
        self.far[1].wait_recv()
        self.near.append(self.send(links.xo, self.b, links.sib))
        for copy in self.near:
            copy.wait_recv()


def reduce_scatter(links, product, part, near, relay, from_left, from_right, fillers=()):
    chips, _, rows, cols = part.shape
    half = cols // 2
    width = half // STEPS
    x, c, xr, xl, xo = links.x, links.c, links.xr, links.xl, links.xo
    fillers = list(fillers)
    swap, first, last = [None] * STEPS, [None] * STEPS, []
    for step in range(STEPS + 2):
        if step < STEPS:
            swap[step] = []
            for base in (step * width, half + step * width):
                span = pl.ds(base, width)
                part[:, :, :, span] = product(base, width).reshape(chips, CORES, rows, width)
                swap[step].append(links.copy(part.at[:, 1 - c, :, span], near.at[:, :, span], links.sib))
        elif fillers:
            fillers.pop(0)()
        if 0 <= step - 1 < STEPS:
            done = step - 1
            span_a, span_b = pl.ds(done * width, width), pl.ds(half + done * width, width)
            for copy, span in zip(swap[done], (span_a, span_b)):
                copy.wait_recv()
                part[:, c, :, span] = part[:, c, :, span] + near[:, :, span]
            first[done] = (
                links.copy(part.at[xo, c, :, span_a], relay.at[0, :, pl.ds(done * width, width)], links.right),
                links.copy(part.at[xo, c, :, span_b], relay.at[1, :, pl.ds(done * width, width)], links.left))
            last.append(links.copy(part.at[xr, c, :, span_b], from_left.at[:, span_b], links.right))
            last.append(links.copy(part.at[xl, c, :, span_a], from_right.at[:, span_a], links.left))
        if 0 <= step - 2 < STEPS:
            done = step - 2
            span_a, span_b = pl.ds(done * width, width), pl.ds(half + done * width, width)
            first[done][0].wait_recv()
            part[xr, c, :, span_a] = part[xr, c, :, span_a] + relay[0, :, pl.ds(done * width, width)]
            last.append(links.copy(part.at[xr, c, :, span_a], from_left.at[:, span_a], links.right))
            first[done][1].wait_recv()
            part[xl, c, :, span_b] = part[xl, c, :, span_b] + relay[1, :, pl.ds(done * width, width)]
            last.append(links.copy(part.at[xl, c, :, span_b], from_right.at[:, span_b], links.left))
    for filler in fillers:
        filler()
    for copy in last:
        copy.wait_recv()
    total = part[x, c] + from_left[...] + from_right[...]
    return total


def rms_norm(hidden, gain):
    hidden_f = hidden.astype(F32)
    inv_rms = lax.rsqrt(jnp.mean(hidden_f * hidden_f, axis=-1, keepdims=True) + NORM_EPS)
    return (hidden_f * inv_rms * gain).astype(BF16)


def rms_norm_pull(hidden, gain, cotangent):
    hidden_f, cot = hidden.astype(F32), cotangent.astype(F32)
    inv_rms = lax.rsqrt(jnp.mean(hidden_f * hidden_f, axis=-1, keepdims=True) + NORM_EPS)
    scaled = cot * gain
    dot = jnp.mean(scaled * hidden_f, axis=-1, keepdims=True)
    d_hidden = scaled * inv_rms - hidden_f * (inv_rms * inv_rms * inv_rms * dot)
    return d_hidden.astype(BF16), jnp.sum(cot * (hidden_f * inv_rms), axis=0, keepdims=True)


def flat(ref):
    chips, cores, rows, cols = ref.shape
    return ref[...].reshape(chips * cores * rows, cols)


def project(full, weight, out, tile):
    def body(index, carry):
        cols = pl.ds(pl.multiple_of(index * tile, tile), tile)
        out[:, cols] = dot_nn(flat(full), weight[:, cols]).astype(BF16)
        return carry
    lax.fori_loop(0, out.shape[1] // tile, body, 0)


def project_t(full, weight, out, tile):
    def body(index, carry):
        span = pl.ds(pl.multiple_of(index * tile, tile), tile)
        out[:, span] = dot_nt(flat(full), weight[span, :]).astype(BF16)
        return carry
    lax.fori_loop(0, out.shape[1] // tile, body, 0)


def head(ref, index):
    return ref[:, index * HEAD_DIM:(index + 1) * HEAD_DIM]


def attention(qkv, heads_out, probs=None):
    group = heads_out.shape[1] // HEAD_DIM
    seq = qkv.shape[0]
    causal = lax.broadcasted_iota(jnp.int32, (seq, seq), 0) >= lax.broadcasted_iota(jnp.int32, (seq, seq), 1)
    for index in range(group):
        scores = dot_nt(head(qkv, index), head(qkv, group)) * HEAD_DIM ** -0.5
        scores = jnp.where(causal, scores, -1e30)
        weight = jnp.exp(scores - jnp.max(scores, axis=-1, keepdims=True))
        prob = weight / jnp.sum(weight, axis=-1, keepdims=True)
        if probs is not None:
            probs[index] = prob
        heads_out[:, index * HEAD_DIM:(index + 1) * HEAD_DIM] = dot_nn(prob.astype(BF16), head(qkv, group + 1)).astype(BF16)


def attention_pull(qkv, probs, d_heads, d_qkv):
    group = d_heads.shape[1] // HEAD_DIM
    d_keys = d_values = None
    for index in range(group):
        d_out, prob = head(d_heads, index), probs[index]
        d_prob = dot_nt(d_out, head(qkv, group + 1))
        d_value = dot_tn(prob.astype(BF16), d_out)
        d_score = (prob * (d_prob - jnp.sum(d_prob * prob, axis=-1, keepdims=True)) * HEAD_DIM ** -0.5).astype(BF16)
        d_qkv[:, index * HEAD_DIM:(index + 1) * HEAD_DIM] = dot_nn(d_score, head(qkv, group)).astype(BF16)
        d_key = dot_tn(d_score, head(qkv, index))
        d_keys = d_key if d_keys is None else d_keys + d_key
        d_values = d_value if d_values is None else d_values + d_value
    d_qkv[:, group * HEAD_DIM:(group + 1) * HEAD_DIM] = d_keys.astype(BF16)
    d_qkv[:, (group + 1) * HEAD_DIM:(group + 2) * HEAD_DIM] = d_values.astype(BF16)


def load(src, dst, sem):
    copy = pltpu.make_async_copy(src, dst, sem)
    copy.start()
    return copy


def forward_kernel(layer, chips, hidden, gain_attn, gain_mlp, w_qkv, w_out, w_gate, w_up, w_down, out,
                   wq, wo, wg, wu, wd, full_in, full_mid, qkv, heads_out, gate, part, near, relay, from_left, from_right,
                   load_sem, send_sem, recv_sem):
    links = Links(chips, send_sem, recv_sem)
    pairs = ((w_qkv, wq), (w_out, wo), (w_gate, wg), (w_up, wu), (w_down, wd))
    loads = [load(src.at[layer], dst, load_sem.at[index]) for index, (src, dst) in enumerate(pairs)]
    row = pl.ds(layer, 1)
    full_in[links.x, links.c] = rms_norm(hidden[...], gain_attn[row, :])
    links.enter((links.right, links.left, links.sib))
    gather = Gather(links, full_in)
    gather.relay()
    gather.finish()
    loads[0].wait()
    project(full_in, wq, qkv, HEAD_DIM)
    attention(qkv, heads_out)
    loads[1].wait()
    total = reduce_scatter(links, lambda col, width: dot_nn(heads_out[...], wo[:, pl.ds(col, width)]),
                           part, near.at[0], relay.at[0], from_left.at[0], from_right.at[0])
    hidden_mid = hidden[...] + total.astype(BF16)
    full_mid[links.x, links.c] = rms_norm(hidden_mid, gain_mlp[row, :])
    out[...] = hidden_mid
    links.drain()
    gather = Gather(links, full_mid)
    gather.relay()
    gather.finish()
    for copy in loads[2:]:
        copy.wait()
    tile = 2 * HEAD_DIM

    def body(index, carry):
        cols = pl.ds(pl.multiple_of(index * tile, tile), tile)
        gate_act = dot_nn(flat(full_mid), wg[:, cols]).astype(BF16).astype(F32)
        up_act = dot_nn(flat(full_mid), wu[:, cols]).astype(BF16).astype(F32)
        gate[:, cols] = (gate_act * jax.nn.sigmoid(gate_act) * up_act).astype(BF16)
        return carry
    lax.fori_loop(0, gate.shape[1] // tile, body, 0)
    total = reduce_scatter(links, lambda col, width: dot_nn(gate[...], wd[:, pl.ds(col, width)]),
                           part, near.at[1], relay.at[1], from_left.at[1], from_right.at[1])
    out[...] = out[...] + total.astype(BF16)
    links.drain()


def backward_kernel(layer, chips, final, hidden, d_out, gain_attn, gain_mlp, w_qkv, w_out, w_gate, w_up, w_down, carried,
                    d_hidden, gains, o_in, o_mid, o_down, o_attn, o_act, o_gate, o_up, o_heads, o_qkv,
                    wq, wo, wg, wu, wd, full_in, full_mid, full_down, full_attn, qkv, heads_out, act, d_gate, d_up, d_heads, d_qkv,
                    probs, part, near, relay, from_left, from_right, gain_mid, gain_last,
                    load_sem, save_sem, send_sem, recv_sem):
    links = Links(chips, send_sem, recv_sem)
    x, c = links.x, links.c
    pairs = ((w_qkv, wq), (w_out, wo), (w_gate, wg), (w_up, wu), (w_down, wd))
    loads = [load(src.at[layer], dst, load_sem.at[index]) for index, (src, dst) in enumerate(pairs)]
    saves = []

    def save(src, dst):
        saves.append(load(src, dst, save_sem.at[len(saves)]))

    row = pl.ds(layer, 1)
    full_in[x, c] = rms_norm(hidden[...], gain_attn[row, :])
    full_down[x, c] = d_out[...]
    links.enter(links.others() if final else (links.right, links.left, links.sib))
    gather = Gather(links, full_in)
    gather_down = Gather(links, full_down)
    gather.relay()
    gather.finish()
    loads[0].wait()
    project(full_in, wq, qkv, HEAD_DIM)
    gather_down.relay()
    attention(qkv, heads_out, probs)
    gather_down.finish()
    save(full_in, o_in)
    save(full_down, o_down)
    save(heads_out, o_heads)
    loads[1].wait()

    def gated():
        loads[4].wait()
        project_t(full_down, wd, act, 2 * HEAD_DIM)

    total = reduce_scatter(links, lambda col, width: dot_nn(heads_out[...], wo[:, pl.ds(col, width)]),
                           part, near.at[0], relay.at[0], from_left.at[0], from_right.at[0], [gated])
    hidden_mid = hidden[...] + total.astype(BF16)
    d_hidden[...] = hidden_mid
    full_mid[x, c] = rms_norm(hidden_mid, gain_mlp[row, :])
    links.drain()
    gather = Gather(links, full_mid)
    gather.relay()
    gather.finish()
    save(full_mid, o_mid)
    loads[2].wait()
    loads[3].wait()
    tile = 2 * HEAD_DIM

    def body(index, carry):
        cols = pl.ds(pl.multiple_of(index * tile, tile), tile)
        gate_act = dot_nn(flat(full_mid), wg[:, cols]).astype(BF16).astype(F32)
        up_act = dot_nn(flat(full_mid), wu[:, cols]).astype(BF16).astype(F32)
        sig = jax.nn.sigmoid(gate_act)
        silu = gate_act * sig
        d_act = act[:, cols].astype(F32)
        d_up[:, cols] = (d_act * silu).astype(BF16)
        d_gate[:, cols] = (d_act * up_act * (sig + silu * (1.0 - sig))).astype(BF16)
        act[:, cols] = (silu * up_act).astype(BF16)
        return carry
    lax.fori_loop(0, act.shape[1] // tile, body, 0)
    save(act, o_act)
    save(d_gate, o_gate)
    save(d_up, o_up)

    def mid_product(col, width):
        return dot_nt(d_gate[...], wg[pl.ds(col, width), :]) + dot_nt(d_up[...], wu[pl.ds(col, width), :])

    total = reduce_scatter(links, mid_product, part, near.at[1], relay.at[1], from_left.at[1], from_right.at[1])
    d_norm, d_gain = rms_norm_pull(d_hidden[...], gain_mlp[row, :], total.astype(BF16))
    d_mid = d_out[...] + d_norm
    full_attn[x, c] = d_mid
    d_hidden[...] = d_mid
    links.drain()
    gather = Gather(links, full_attn)
    lanes = gain_mid.shape[2]
    done = carried.shape[0] if final else 0

    def put(ref, index, value):
        for line in range(lanes):
            ref[index, line:line + 1, :] = value[:, line * HEAD_DIM:(line + 1) * HEAD_DIM]

    mine = gain_mid.at[links.me]
    if final:
        mine[0:done] = carried[...]
    put(mine, done, d_gain)
    gather.relay()
    gather.finish()
    save(full_attn, o_attn)
    shares = []
    if final:
        shares = [links.copy(mine, mine, peer) for peer in links.others()]
    project_t(full_attn, wo, d_heads, HEAD_DIM)
    attention_pull(qkv, probs, d_heads, d_qkv)
    save(d_qkv, o_qkv)
    total = reduce_scatter(links, lambda col, width: dot_nt(d_qkv[...], wq[pl.ds(col, width), :]),
                           part, near.at[2], relay.at[2], from_left.at[2], from_right.at[2])
    d_norm, d_gain = rms_norm_pull(hidden[...], gain_attn[row, :], total.astype(BF16))
    mine_last = gain_last.at[links.me]
    put(mine_last, 0, d_gain)
    if final:
        shares += [links.copy(mine_last, mine_last, peer) for peer in links.others()]
    d_hidden[...] = d_hidden[...] + d_norm
    if final:
        for copy in shares:
            copy.wait_recv()
        size = chips * CORES
        gains[0:done + 1] = sum([gain_mid[peer] for peer in range(1, size)], gain_mid[0])
        gains[done + 1:done + 2] = sum([gain_last[peer] for peer in range(1, size)], gain_last[0])
    else:
        gains[0:1] = mine[...]
        gains[1:2] = mine_last[...]
    for copy in saves:
        copy.wait()
    links.drain()


def grads_kernel(layer, fresh, *refs):
    ins, rest = refs[:9], refs[9:]
    if not fresh:
        rest = rest[5:]
    outs, rest = rest[:5], rest[5:]
    full_in, full_mid, full_down, full_attn, act, d_gate, d_up, heads_out, d_qkv = rest[:9]
    stage, load_sem, save_sem = rest[9:]
    loads = [load(src, dst, load_sem.at[index]) for index, (src, dst) in enumerate(zip(ins, rest[:9]))]
    tile = stage.shape[1]
    wide = 1024
    jobs = ((act, full_down, outs[4], (4, 2)), (full_mid, d_gate, outs[2], (1, 5)), (full_mid, d_up, outs[3], (6,)),
            (heads_out, full_attn, outs[1], (7, 3)), (full_in, d_qkv, outs[0], (0, 8)))
    for left, right, out, needs in jobs:
        for index in needs:
            loads[index].wait()
        rows, cols = out.shape[1], out.shape[2]
        size = min(tile, rows)
        if rows % size:
            size = size // 2
        count = rows // size

        def slot_copy(slot, start, size=size, cols=cols, out=out):
            return pltpu.make_async_copy(stage.at[slot, pl.ds(0, size), pl.ds(0, cols)],
                                         out.at[layer, pl.ds(start, size), :], save_sem.at[slot])

        def body(index, carry, left=left, right=right, size=size, cols=cols, slot_copy=slot_copy):
            slot = lax.rem(index, 2)
            start = pl.multiple_of(index * size, size)

            @pl.when(index >= 2)
            def _():
                slot_copy(slot, start).wait()
            span = pl.ds(start, size)
            if len(left.shape) == 4:
                chips, cores, some, _ = left.shape
                turned = left[:, :, :, span].reshape(chips * cores * some, size)
            else:
                turned = left[:, span]
            turned = turned.T
            for col in range(0, cols, wide):
                width = min(wide, cols - col)
                if len(right.shape) == 4:
                    chips, cores, some, _ = right.shape
                    piece = right[:, :, :, col:col + width].reshape(chips * cores * some, width)
                else:
                    piece = right[:, col:col + width]
                stage[slot, 0:size, col:col + width] = dot_nn(turned, piece).astype(BF16)
            slot_copy(slot, start).start()
            return carry
        lax.fori_loop(0, count, body, 0)
        for slot in range(min(2, count)):
            slot_copy(slot, 0).wait()


def vmem(*shape, dtype=BF16):
    return pltpu.VMEM(shape, dtype)


def solution(mesh):
    chips = mesh.shape['tp'] // CORES
    row_spec = P(('dp', 'tp'), None)
    col_spec = P(None, None, 'tp')
    mid_spec = P(None, 'tp', None)
    in_specs = (row_spec, row_spec, P(None, None), P(None, None), col_spec, mid_spec, col_spec, col_spec, mid_spec)
    out_specs = (row_spec, row_spec, P('dp', None, 'tp'), P('dp', 'tp', None), P('dp', None, 'tp'), P('dp', None, 'tp'), P('dp', 'tp', None), P('dp', None), P('dp', None))

    def device_step(x, grad_y, gain_attn, gain_mlp, w_qkv, w_out, w_gate, w_up, w_down):
        layers, width, qkv_cols = w_qkv.shape
        head_cols, units, rows = w_out.shape[1], w_gate.shape[2], x.shape[0]
        group = head_cols // HEAD_DIM
        seq = chips * CORES * rows
        lanes = width // HEAD_DIM
        full = (chips, CORES, rows, width)
        weights = (w_qkv, w_out, w_gate, w_up, w_down)
        weight_bufs = [vmem(*weight.shape[1:]) for weight in weights]

        def ring_bufs(uses):
            return [vmem(*full, dtype=F32), vmem(uses, chips, rows, width, dtype=F32), vmem(uses, 2, rows, width // 2, dtype=F32),
                    vmem(uses, rows, width, dtype=F32), vmem(uses, rows, width, dtype=F32)]

        def dma(count):
            return pltpu.SemaphoreType.DMA((count,))

        def params(ident):
            return pltpu.CompilerParams(collective_id=ident, has_side_effects=True, vmem_limit_bytes=VMEM_LIMIT)

        def forward(layer, hidden):
            copies = 2 * 13 + 2 * 8 * STEPS
            return pl.pallas_call(
                functools.partial(forward_kernel, layer, chips),
                out_shape=jax.ShapeDtypeStruct(hidden.shape, BF16),
                in_specs=[VMEM_SPEC] * 3 + [ANY] * 5,
                out_specs=VMEM_SPEC,
                scratch_shapes=weight_bufs + [vmem(*full), vmem(*full), vmem(seq, qkv_cols), vmem(seq, head_cols), vmem(seq, units)]
                + ring_bufs(2) + [dma(5), dma(copies), dma(copies)],
                compiler_params=params(layer), name=f'forward_{layer}',
            )(hidden, gain_attn, gain_mlp, *weights)

        def backward(layer, hidden, d_out, carried):
            final = layer == 0
            peers = chips * CORES - 1
            copies = 4 * 13 + 3 * 8 * STEPS + 2 * peers
            done = carried.shape[0] if final else 0
            factor = lambda *shape: jax.ShapeDtypeStruct(shape, BF16)
            return pl.pallas_call(
                functools.partial(backward_kernel, layer, chips, final),
                out_shape=[factor(*hidden.shape), jax.ShapeDtypeStruct((done + 2, lanes, HEAD_DIM), F32)] + [factor(*full)] * 4
                + [factor(seq, units)] * 3 + [factor(seq, head_cols), factor(seq, qkv_cols)],
                in_specs=[VMEM_SPEC] * 4 + [ANY] * 5 + [VMEM_SPEC],
                out_specs=[VMEM_SPEC] * 2 + [ANY] * 9,
                scratch_shapes=weight_bufs + [vmem(*full)] * 4
                + [vmem(seq, qkv_cols), vmem(seq, head_cols), vmem(seq, units), vmem(seq, units), vmem(seq, units),
                   vmem(seq, head_cols), vmem(seq, qkv_cols), vmem(group, seq, seq, dtype=F32)] + ring_bufs(3)
                + [vmem(chips * CORES, done + 1, lanes, HEAD_DIM, dtype=F32), vmem(chips * CORES, 1, lanes, HEAD_DIM, dtype=F32),
                   dma(5), dma(9), dma(copies), dma(copies)],
                compiler_params=params(layers + layer), name=f'backward_{layer}',
            )(hidden, d_out, gain_attn, gain_mlp, *weights, carried)

        grad_shapes = [jax.ShapeDtypeStruct(weight.shape, BF16) for weight in weights]

        def grads(layer, factors, into):
            given = [] if into is None else list(into)
            return pl.pallas_call(
                functools.partial(grads_kernel, layer, into is None),
                out_shape=grad_shapes,
                in_specs=[ANY] * (len(factors) + len(given)),
                out_specs=[ANY] * 5,
                scratch_shapes=[vmem(*factor.shape) for factor in factors] + [vmem(2, 256, width), dma(len(factors)), dma(2)],
                input_output_aliases={len(factors) + index: index for index in range(len(given))},
                compiler_params=pltpu.CompilerParams(vmem_limit_bytes=VMEM_LIMIT), name=f'grads_{layer}',
            )(*factors, *given)

        kept = [x]
        for layer in range(layers):
            kept.append(forward(layer, kept[-1]))
        d_hidden, out_grads, partial_gains = grad_y, None, []
        for layer in reversed(range(layers)):
            carried = jnp.concatenate(partial_gains) if partial_gains else jnp.zeros((1, lanes, HEAD_DIM), F32)
            d_hidden, gains, *factors = backward(layer, kept[layer], d_hidden, carried)
            partial_gains.append(gains)
            out_grads = grads(layer, factors, out_grads)
            d_hidden, *out_grads = lax.optimization_barrier((d_hidden, *out_grads))
        order = gains.reshape(layers, 2, width)[::-1]
        return (kept[-1], d_hidden, *out_grads, order[:, 1], order[:, 0])

    return jax.shard_map(device_step, mesh=mesh, in_specs=in_specs, out_specs=out_specs, check_vma=False)
```

time: 722 us -> 448 us (0.62)
  waiting for transfers between devices: 445 us -> 0 us
  Pallas kernels: 0 us -> 423 us
  matrix products: 165 us -> 0 us
  other arithmetic: 55.7 us -> 0 us
  blocking collectives: 24 us -> 0 us
  between operations: 15.4 us -> 1.19 us
  local copies, waits for them, and re-layouts: 4.74 us -> 16 us
    pallas_call x0 -> x6, Pallas kernels: none -> 423 us  [the longest x2 224 us: backward(): pl.pallas_call(functools.partial(backward_kernel, layer, chips, final), o...]
    reduce_scatter x10 -> x0, waiting for transfers between devices: 243 us -> none  [scatter_rows(): lax.psum_scatter(part_sum, 'tp', scatter_dimension=0, tiled=True)]
    all_gather x12 -> x0, waiting for transfers between devices: 200 us -> none  [gather_rows(): return lax.all_gather(row_shard, 'tp', axis=0, tiled=True)]
    dot_general x52 -> x0, matrix products: 165 us -> none  [the longest x36 80.9 us: contract(): jnp.einsum(eq_form, left_op, right_op, preferred_element_type=jnp.float32)]
    another operation x8 -> x0, other arithmetic: 25.3 us -> none  [the longest x4 24.9 us: device_step(): jnp.stack([grads[kind_idx] for grads in layer_grads])]
    psum x1 -> x0, blocking collectives: 24 us -> none  [device_step(): gain_grads = lax.psum(jnp.stack([stacked[0], stacked[1]]), 'tp')]
    reduce_sum x16 -> x0, other arithmetic: 14.4 us -> none  [the longest x8 7.19 us: rms_norm(): jnp.mean(hidden_f * hidden_f, axis=-1, keepdims=True) + NORM_EPS]
    slice x2 -> x3, local copies, waits for them, and re-layouts: 0.86 us -> 14 us  [device_step(): return (kept[-1], d_hidden, *out_grads, order[:, 1], order[:, 0])]
  transfers between devices with their start and end apart: 22 -> 0, of which waited for: 20 -> 0; matrix products, arithmetic and copies ran while one was open for 19% -> 0% of each run, Pallas kernels for 0% -> 0%
where the time goes in v1:
time: 448 us; the launch traced here: 440 us
  Pallas kernels  423 us (94%)
  local copies, waits for them, and re-layouts  16 us (4%)
    pallas_call x2, Pallas kernels, backward(): pl.pallas_call(functools.partial(backward_kernel, layer, chips, final), o...  224 us
    pallas_call x2, Pallas kernels, forward(): pl.pallas_call(functools.partial(forward_kernel, layer, chips), out_shape...  139 us
    pallas_call x2, Pallas kernels, grads(): pl.pallas_call(functools.partial(grads_kernel, layer, into is None), out_...  60.5 us
    slice x3, local copies, waits for them, and re-layouts, device_step(): return (kept[-1], d_hidden, *out_grads, order[:, 1], order[:, 0])  14 us

profile of v1, /device:TPU:112, one launch (start us, length us, event | category | flops | bytes accessed | tf_op | source)
XLA Modules:
  0.0 439.9 jit_solution(17742275446071447821)
XLA Ops:
  0.6 69.9 %forward_0.1.hidden = bf16[32,3072]{1,0:T(8,128)(2,1)} custom-call(bf16[32,3072]{1,0:T(8,128)(2,1)} %hidden.3, f32[2,3072]{1,0:T(2,128)} %gain_attn.7, f32[2,3072]{1,0:T(2,128)} %gain_mlp.7, bf16[2,3072,640]{2,1,0:T(8,128)(2,1)} %w_qkv.7, bf16[2,384,3072]{2,1,0:T(8,128)(2,1)} %w_out.7, bf16[2,3072,1024]{2,1,0:T(8,128)(2,1)} %w_gate.7, ...), custom_call_target="tpu_custom_call" | custom-call | tf_op jit(solution)/shard_map/forward_0/pallas_call | solution.py:482
  70.5 68.7 %forward_1.1 = bf16[32,3072]{1,0:T(8,128)(2,1)} custom-call(bf16[32,3072]{1,0:T(8,128)(2,1)} %forward_0.1.hidden, f32[2,3072]{1,0:T(2,128)} %gain_attn.7, f32[2,3072]{1,0:T(2,128)} %gain_mlp.7, bf16[2,3072,640]{2,1,0:T(8,128)(2,1)} %w_qkv.7, bf16[2,384,3072]{2,1,0:T(8,128)(2,1)} %w_out.7, bf16[2,3072,1024]{2,1,0:T(8,128)(2,1)} %w_gate.7, ...), custom_call_target="tpu_custom_call" | custom-call | tf_op jit(solution)/shard_map/forward_1/pallas_call | solution.py:482
  139.2 0.6 broadcast_in_dim.3.carried
  139.8 108.7 %backward_1.1 = (bf16[32,3072]{1,0:T(8,128)(2,1)}, f32[2,24,128]{2,1,0:T(8,128)}, bf16[4,2,32,3072]{3,2,1,0:T(8,128)(2,1)}, bf16[4,2,32,3072]{3,2,1,0:T(8,128)(2...) custom-call(bf16[32,3072]{1,0:T(8,128)(2,1)} %forward_0.1.hidden, ...), custom_call_target="tpu_custom_call" | custom-call | tf_op jit(solution)/shard_map/backward_1/pallas_call | solution.py:498
  248.5 30.2 %grads_1.1 = (bf16[2,3072,640]{2,1,0:T(8,128)(2,1)}, bf16[2,384,3072]{2,1,0:T(8,128)(2,1)}, bf16[2,3072,1024]{2,1,0:T(8,128)(2,1)}, bf16[2,3072,1024]{2,1,0:T(8,128)(2,1)}, bf16[2,1024,3072]{2,1,0:T(8,128)(2,1)}) custom-call(bf16[4,2,32,3072]{3,2,1,0:T(8,128)(2,1)} %get-tuple-element.54.refs_0_, bf16[4,2,32,3072]{3,2,1,0:T(8,128)(2,1)} %get-tuple-element.55.refs_1_, ...), custom_call_target="tpu_custom_call" | custom-call | tf_op jit(solution)/shard_map/grads_1/pallas_call | solution.py:516
  278.7 114.9 %backward_0.1 = (bf16[32,3072]{1,0:T(8,128)(2,1)}, f32[4,24,128]{2,1,0:T(8,128)}, bf16[4,2,32,3072]{3,2,1,0:T(8,128)(2,1)}, bf16[4,2,32,3072]{3,2,1,0:T(8,128)(2...) custom-call(bf16[32,3072]{1,0:T(8,128)(2,1)} %hidden.3, ...), custom_call_target="tpu_custom_call" | custom-call | tf_op jit(solution)/shard_map/backward_0/pallas_call | solution.py:498
  393.6 0.0 copy-start.2
  393.6 0.0 copy-start
  393.7 0.0 copy-start.1
  393.7 30.3 %grads_0.1 = (bf16[2,3072,640]{2,1,0:T(8,128)(2,1)}, bf16[2,384,3072]{2,1,0:T(8,128)(2,1)}, bf16[2,3072,1024]{2,1,0:T(8,128)(2,1)}, bf16[2,3072,1024]{2,1,0:T(8,128)(2,1)}, bf16[2,1024,3072]{2,1,0:T(8,128)(2,1)}) custom-call(bf16[4,2,32,3072]{3,2,1,0:T(8,128)(2,1)} %get-tuple-element.7, ...), custom_call_target="tpu_custom_call", output_to_operand_aliasing={{0}: (9, {}), {1}: (10, {}), {2}: (11, {}), {3}: (12, {}), ... | custom-call | tf_op jit(solution)/shard_map/grads_0/pallas_call | solution.py:516
  424.0 0.0 copy-done.2
  424.1 7.0 %slice.15 = f32[2,1,3072]{2,0,1:T(2,128)} reverse(f32[2,1,3072]{2,0,1:T(2,128)S(1)} %copy.26), dimensions={0} | reverse | bytes 49152 | tf_op jit(solution)/shard_map/slice | solution.py:537
  431.1 7.0 %slice.13 = f32[2,1,3072]{2,0,1:T(2,128)} reverse(f32[2,1,3072]{2,0,1:T(2,128)S(1)} %copy.25), dimensions={0} | reverse | bytes 49152 | tf_op jit(solution)/shard_map/slice | solution.py:537
  438.1 0.0 copy-done
  438.1 0.7 copy.34
  438.8 0.0 copy-done.1
  438.8 0.7 copy.35
  (4 shorter events, 0.1 us)
Async XLA Ops:
  393.6 30.3 %copy-start.2 = (f32[4,24,128]{2,1,0:T(8,128)S(1)}, f32[4,24,128]{2,1,0:T(8,128)}, u32[]{:S(2)}) copy-start(f32[4,24,128]{2,1,0:T(8,128)} %get-tuple-element.96) | copy-start | bytes 147460
  393.6 44.4 %copy-start = (bf16[32,3072]{1,0:T(8,128)(2,1)S(1)}, bf16[32,3072]{1,0:T(8,128)(2,1)}, u32[]{:S(2)}) copy-start(bf16[32,3072]{1,0:T(8,128)(2,1)} %forward_1.1) | copy-start | bytes 589828
  393.7 45.1 %copy-start.1 = (bf16[32,3072]{1,0:T(8,128)(2,1)S(1)}, bf16[32,3072]{1,0:T(8,128)(2,1)}, u32[]{:S(2)}) copy-start(bf16[32,3072]{1,0:T(8,128)(2,1)} %get-tuple-element.109) | copy-start | bytes 589828
